TPU v7x, 32 devices: a whole 2x2x4 slice. The times are simulated.
32 devices in a mesh: cell: 16 (over z, y, x), gene: 2 (over core).
Axes of the slice: x: 2, y: 2, z: 4, core: 2. Of those that a mesh axis runs over, the one named last changes fastest.
Arguments:
- tiles: bfloat16 [2, 1024, 128, 128], P('gene', 'cell'), may hold values from -8 to 8
- tile_row: int32 [2, 1024], P('gene', 'cell'), may hold values from 0 to 7, as said below
- tile_col: int32 [2, 1024], P('gene', 'cell'), may hold values from 0 to 15
- tile_count: int32 [2, 16], P('gene', 'cell'), may hold values from 1 to 64, as said below
- start_basis: bfloat16 [64, 4096], P(None, 'gene'), may hold values from -0.09375 to 0.09375
Outputs:
- basis: bfloat16 [64, 16384], P(None, 'cell')
- loadings: float32 [64, 4096], P(None, ('gene', 'cell'))
Inputs may be any that keep to these rules, and one draw needn't show every extreme that they name: `tile_row`: tile row of each slot, within 0 to 7; the slots of one device name distinct (row, column) pairs. `tile_count`: slots in use; for each index of gene some device uses all 64.
All inputs are finite; a program needn't handle non-finite values.
Results may differ from a plain program's by a relative error of at most 0.018.
Values may be sent and summed in bfloat16 or wider, within the bound.
No kernel may reach another device: no remote copies, remote signals or barrier semaphores. Data moves between devices by JAX's collectives and lax.ppermute only.
A program may use at most 64 MiB of HBM per device.

v0:
```python
import jax
import jax.numpy as jnp
from jax import lax
from jax.sharding import PartitionSpec as P

ROW_BLOCKS = 8


def solve_lower(lower, right):
    return lax.linalg.triangular_solve(lower, right, left_side=True, lower=True)


def gram_of(scores):
    return jnp.dot(
        scores, scores.T, precision=lax.Precision.HIGHEST, preferred_element_type=jnp.float32
    )


def orthonormal(scores, first_total):
    first = first_total(gram_of(scores))
    lower_one = jnp.linalg.cholesky(first)
    return solve_lower(lower_one, scores)


def local(tiles, tile_row, tile_col, tile_count, start_basis):
    blocks_local = tiles[0]
    slot_count = blocks_local.shape[0]
    tile_size = blocks_local.shape[-1]
    width = start_basis.shape[0]
    gene_dev = start_basis.shape[1]
    gene_blocks = gene_dev // tile_size
    row_blocks = ROW_BLOCKS
    cell_dev = row_blocks * tile_size
    row_index = tile_row[0]
    col_index = tile_col[0]
    live = jnp.arange(slot_count) < tile_count[0, 0]
    row_target = jnp.where(live, row_index, row_blocks)
    col_target = jnp.where(live, col_index, gene_blocks)

    def first_total(gram):
        return lax.psum(gram, ("cell", "gene"))

    def merge_halves(partial_scores):
        return lax.psum_scatter(partial_scores, "gene", scatter_dimension=1, tiled=True)

    def scores_of(basis):
        picked = jnp.take(basis.reshape(width, gene_blocks, tile_size), col_index, axis=1)
        products = jnp.einsum(
            "ksg,srg->skr", picked, blocks_local, preferred_element_type=jnp.float32
        )
        summed = jax.ops.segment_sum(products, row_target, num_segments=row_blocks + 1)[:row_blocks]
        return merge_halves(jnp.transpose(summed, (1, 0, 2)).reshape(width, cell_dev))

    def loadings_of(ortho_half):
        picked = jnp.take(ortho_half.reshape(width, row_blocks, tile_size), row_index, axis=1)
        products = jnp.einsum(
            "ksr,srg->skg", picked, blocks_local, preferred_element_type=jnp.float32
        )
        summed = jax.ops.segment_sum(products, col_target, num_segments=gene_blocks + 1)[
            :gene_blocks
        ]
        return jnp.transpose(summed, (1, 0, 2)).reshape(width, gene_dev)

    ortho = orthonormal(scores_of(start_basis), first_total)
    ortho_half = ortho.astype(jnp.bfloat16)
    ortho_rows = lax.all_gather(ortho_half, "gene", axis=1, tiled=True)
    partial_value = loadings_of(ortho_rows)
    next_basis = lax.psum(partial_value, "cell").astype(jnp.bfloat16)
    ortho_two = orthonormal(scores_of(next_basis), first_total)
    scale = jnp.sqrt(jnp.float32(lax.axis_size("cell") * cell_dev))
    ortho_two_half = ortho_two.astype(jnp.bfloat16)
    basis_piece = (ortho_two * scale).astype(jnp.bfloat16)
    final_rows, basis = (
        lax.all_gather(ortho_two_half, "gene", axis=1, tiled=True),
        lax.all_gather(basis_piece, "gene", axis=1, tiled=True),
    )
    loadings = lax.psum_scatter(loadings_of(final_rows), "cell", scatter_dimension=1, tiled=True)
    return (basis, loadings)


def solution(mesh):
    return jax.shard_map(
        local,
        mesh=mesh,
        in_specs=(
            P("gene", "cell", None, None),
            P("gene", "cell"),
            P("gene", "cell"),
            P("gene", "cell"),
            P(None, "gene"),
        ),
        out_specs=(P(None, "cell"), P(None, ("gene", "cell"))),
        check_vma=False,
    )
```

profile of v0, /device:TPU:0, one launch (start us, length us, event | category | flops | bytes accessed | tf_op | source)
XLA Modules:
  0.0 349.9 jit_solution(15291023441210544630)
XLA Ops:
  7.2 0.0 copy-start
  7.2 0.0 copy-start.1
  7.2 0.0 copy-start.2
  7.2 0.0 reduce-scatter.4.cloned.1.call-start
  7.2 0.8 compare_select_fusion
  8.0 0.7 compare_and_fusion
  8.7 1.0 copy_bitcast_fusion.5
  10.4 0.7 gather_fusion
  11.1 0.0 copy-done.1
  11.2 0.0 copy-done.2
  11.2 0.0 copy-done
  11.2 2.9 fusion.6
  14.1 7.1 %scatter_fusion = f32[9,64,128]{2,1,0:T(8,128)S(1)} fusion(f32[9,64,128]{2,1,0:T(8,128)S(1)} %broadcast.69.clone, s32[64]{0:T(128)S(1)} %get-tuple-element.8, f32[64,64,128]{2,1,0:T(8,128)} %fusion.6), kind=kCustom, calls=%fused_computation.4 | custom fusion | flops 524288 | bytes 6291712 | tf_op jit(solution)/shard_map/scatter-add | solution.py:51
  21.2 0.7 copy_bitcast_fusion.3
  21.9 0.0 reduce-scatter.4.cloned.1.call-update
  21.9 0.0 reduce-scatter.6.cloned.1.call-start
  22.0 10.5 %reduce-scatter.4.cloned.1.call-done = f32[64,512]{1,0:T(8,128)} async-done(((f32[64,1024]{1,0:T(8,128)}), f32[64,512]{1,0:T(8,128)}) %reduce-scatter.4.cloned.1.call-update) | async-done | bytes 131088 | tf_op jit(solution)/shard_map/reduce_scatter | solution.py:44
  32.5 1.2 fusion.40
  33.8 40.5 %psum.21 = f32[64,64]{0,1:T(8,128)S(1)} all-reduce(f32[64,64]{0,1:T(8,128)S(1)} %fusion.40), channel_id=1, replica_groups=mesh['cell'=16,'gene'=2] {'cell','gene'}, use_global_device_ids=true, to_apply=%region_2.4 | all-reduce | flops 4096 | bytes 32768 | tf_op jit(solution)/shard_map/psum | solution.py:41
  74.3 0.1 copy.20
  74.4 5.8 %cholesky.44 = f32[64,64]{1,0:T(8,128)S(1)} custom-call(f32[64,64]{1,0:T(8,128)S(1)} %fusion.30), custom_call_target="Cholesky" | custom-call | tf_op jit(solution)/shard_map/jit(cholesky)/cholesky | solution.py:21
  80.3 0.6 compare_reduce_fusion.1
  80.9 0.7 fusion.24
  81.6 4.9 %custom-call.6 = f32[1,64,64]{1,2,0:T(8,128)S(1)} custom-call(f32[1,64,64]{2,1,0:T(8,128)S(1)} %fusion.24), custom_call_target="InvertDiagBlocksLowerTriangular" | custom-call | tf_op jit(solution)/shard_map/triangular_solve/custom-call.0 | solution.py:10
  86.5 1.2 convolution_convert_fusion
  87.7 1.9 all_gather.9
  89.7 0.7 gather_fusion.1
  90.4 2.1 fusion.4
  92.6 7.1 %scatter_fusion.1 = f32[17,64,128]{2,1,0:T(8,128)S(1)} fusion(f32[17,64,128]{2,1,0:T(8,128)S(1)} %broadcast.70.clone, s32[64]{0:T(128)S(1)} %get-tuple-element.9, f32[64,64,128]{2,1,0:T(8,128)} %fusion.4), kind=kCustom, calls=%fused_computation.5 | custom fusion | flops 524288 | bytes 6291712 | tf_op jit(solution)/shard_map/scatter-add | solution.py:59
  99.7 81.7 %all-reduce.1 = bf16[64,2048]{1,0:T(8,128)(2,1)S(1)} all-reduce(f32[64,2048]{1,0:T(8,128)S(1)} %copy_bitcast_fusion.1), channel_id=1, replica_groups=mesh['cell'=16,'gene'=2] {'cell'}, use_global_device_ids=true, to_apply=%region_6.11 | all-reduce | flops 131072 | bytes 786432 | tf_op jit(solution)/shard_map/psum | solution.py:68
  181.3 0.1 copy_bitcast_fusion.4
  181.4 0.8 gather_fusion.2
  182.2 2.9 fusion.2
  185.1 7.1 %scatter_fusion.2 = f32[9,64,128]{2,1,0:T(8,128)S(1)} fusion(f32[9,64,128]{2,1,0:T(8,128)S(1)} %broadcast.69, s32[64]{0:T(128)S(1)} %get-tuple-element.8, f32[64,64,128]{2,1,0:T(8,128)} %fusion.2), kind=kCustom, calls=%fused_computation.6 | custom fusion | flops 524288 | bytes 6291712 | tf_op jit(solution)/shard_map/scatter-add | solution.py:51
  192.2 0.7 copy_bitcast_fusion.2
  192.9 0.0 reduce-scatter.6.cloned.1.call-update
  192.9 0.0 reduce-scatter.8.cloned.1.call-start
  192.9 4.2 %reduce-scatter.6.cloned.1.call-done = f32[64,512]{1,0:T(8,128)} async-done(((f32[64,1024]{1,0:T(8,128)}), f32[64,512]{1,0:T(8,128)}) %reduce-scatter.6.cloned.1.call-update) | async-done | bytes 131088 | tf_op jit(solution)/shard_map/reduce_scatter | solution.py:44
  197.1 1.2 fusion.41
  198.4 40.8 %psum.23 = f32[64,64]{0,1:T(8,128)S(1)} all-reduce(f32[64,64]{0,1:T(8,128)S(1)} %fusion.41), channel_id=1, replica_groups=mesh['cell'=16,'gene'=2] {'cell','gene'}, use_global_device_ids=true, to_apply=%region_9.14 | all-reduce | flops 4096 | bytes 32768 | tf_op jit(solution)/shard_map/psum | solution.py:41
  239.1 0.1 copy.26
  239.2 5.8 %cholesky.55 = f32[64,64]{1,0:T(8,128)S(1)} custom-call(f32[64,64]{1,0:T(8,128)S(1)} %fusion.28), custom_call_target="Cholesky" | custom-call | tf_op jit(solution)/shard_map/jit(cholesky)/cholesky | solution.py:21
  245.1 0.6 compare_reduce_fusion
  245.8 0.7 fusion.25
  246.4 4.9 %custom-call.7 = f32[1,64,64]{1,2,0:T(8,128)S(1)} custom-call(f32[1,64,64]{2,1,0:T(8,128)S(1)} %fusion.25), custom_call_target="InvertDiagBlocksLowerTriangular" | custom-call | tf_op jit(solution)/shard_map/triangular_solve/custom-call.0 | solution.py:10
  251.3 1.2 fusion.39
  252.6 1.9 all_gather.11
  254.5 0.7 gather_fusion.3
  255.2 2.1 fusion
  257.4 7.1 %scatter_fusion.3 = f32[17,64,128]{2,1,0:T(8,128)S(1)} fusion(f32[17,64,128]{2,1,0:T(8,128)S(1)} %broadcast.70, s32[64]{0:T(128)S(1)} %get-tuple-element.9, f32[64,64,128]{2,1,0:T(8,128)} %fusion), kind=kCustom, calls=%fused_computation.7 | custom fusion | flops 524288 | bytes 6291712 | tf_op jit(solution)/shard_map/scatter-add | solution.py:59
  264.4 0.8 copy_bitcast_fusion
  265.3 0.0 reduce-scatter.8.cloned.1.call-update
  265.3 1.9 all_gather.10
  267.2 75.5 %reduce-scatter.8.cloned.1.call-done = f32[64,128]{1,0:T(8,128)} async-done(((f32[64,2048]{1,0:T(8,128)}), f32[64,128]{1,0:T(8,128)}) %reduce-scatter.8.cloned.1.call-update) | async-done | bytes 32784 | tf_op jit(solution)/shard_map/reduce_scatter | solution.py:77
  342.7 0.7 copy.55
  (16 shorter events, 0.3 us)
Async XLA Ops:
  7.2 4.0 %copy-start = (bf16[1,64,128,128]{3,2,1,0:T(8,128)(2,1)S(1)}, bf16[1,64,128,128]{3,2,1,0:T(8,128)(2,1)}, u32[]{:S(2)}) copy-start(bf16[1,64,128,128]{3,2,1,0:T(8,128)(2,1)} %param.12) | copy-start | bytes 6291460
  7.2 4.0 %copy-start.1 = (s32[1,64]{1,0:T(1,128)S(1)}, s32[1,64]{1,0:T(1,128)}, u32[]{:S(2)}) copy-start(s32[1,64]{1,0:T(1,128)} %param.14) | copy-start | bytes 772
  7.2 4.0 %copy-start.2 = (s32[1,64]{1,0:T(1,128)S(1)}, s32[1,64]{1,0:T(1,128)}, u32[]{:S(2)}) copy-start(s32[1,64]{1,0:T(1,128)} %param.13) | copy-start | bytes 772
  7.2 25.3 %reduce-scatter.4.cloned.1.call-start = ((), (), s32[]{:S(2)}) async-start(), calls=%async_computation.3 | async-start | bytes 393216 | tf_op jit(solution)/shard_map/reduce_scatter | solution.py:44
  21.9 175.2 %reduce-scatter.6.cloned.1.call-start = ((), (), s32[]{:S(2)}) async-start(), calls=%async_computation.4 | async-start | bytes 393216 | tf_op jit(solution)/shard_map/reduce_scatter | solution.py:44
  192.9 149.8 %reduce-scatter.8.cloned.1.call-start = ((), (), s32[]{:S(2)}) async-start(), calls=%async_computation.5 | async-start | bytes 557056 | tf_op jit(solution)/shard_map/reduce_scatter | solution.py:77
Sparse Core Ops, SparseCore 0:
  22.0 10.4 reduce-scatter.3
  193.0 4.0 reduce-scatter.5
  265.4 77.2 reduce-scatter.7
where the time goes:
time: 351 us; the launch traced here: 350 us
  blocking collectives  169 us (48%)
  waiting for transfers between devices  90.3 us (26%)
  other arithmetic  53.9 us (15%)
  matrix products  14.9 us (4%)
  between operations  14.7 us (4%)
  local copies, waits for them, and re-layouts  7.35 us (2%)
    psum x1, blocking collectives, local(): next_basis = lax.psum(partial_value, 'cell').astype(jnp.bfloat16)  81.7 us
    psum x2, blocking collectives, first_total(): return lax.psum(gram, ('cell', 'gene'))  81.3 us
    reduce_scatter x1, waiting for transfers between devices, local(): lax.psum_scatter(loadings_of(final_rows), 'cell', scatter_dimension=1, ti...  75.5 us
    reduce_scatter x2, waiting for transfers between devices, merge_halves(): lax.psum_scatter(partial_scores, 'gene', scatter_dimension=1, tiled=True)  14.7 us
    scatter-add x2, other arithmetic, scores_of(): jax.ops.segment_sum(products, row_target, num_segments=row_blocks + 1)  14.1 us
    scatter-add x2, other arithmetic, loadings_of(): jax.ops.segment_sum(products, col_target, num_segments=gene_blocks + 1)  14.1 us
    another operation x6, other arithmetic, orthonormal(): lower_one = jnp.linalg.cholesky(first)  13 us
    another operation x4, other arithmetic, solve_lower(): return lax.linalg.triangular_solve(lower, right, left_side=True, lower=True)  11.1 us
  transfers between devices with their start and end apart: 3, of which 3 were waited for; matrix products, arithmetic and copies ran while one was open for 0% of the time, Pallas kernels for 0%

commit v1 on v0

--- a/solution.py
+++ b/solution.py
@@ -38,7 +38,7 @@
     col_target = jnp.where(live, col_index, gene_blocks)
 
     def first_total(gram):
-        return lax.psum(gram, ("cell", "gene"))
+        return jnp.sum(lax.all_gather(gram, ("cell", "gene")), axis=0)
 
     def merge_halves(partial_scores):
         return lax.psum_scatter(partial_scores, "gene", scatter_dimension=1, tiled=True)

time: 351 us -> 351 us (level)
  blocking collectives: 169 us -> 173 us
    all_gather x0 -> x2, blocking collectives: none -> 89.3 us  [first_total(): return jnp.sum(lax.all_gather(gram, ('cell', 'gene')), axis=0)]
    psum x2 -> x0, blocking collectives: 81.3 us -> none  [first_total(): return lax.psum(gram, ('cell', 'gene'))]
    psum x1, blocking collectives: 81.7 us -> 77.5 us  [local(): next_basis = lax.psum(partial_value, 'cell').astype(jnp.bfloat16)]
    reduce_scatter x1, waiting for transfers between devices: 75.5 us -> 71.8 us  [local(): lax.psum_scatter(loadings_of(final_rows), 'cell', scatter_dimension=1, ti...]
where the time goes in v1:
time: 351 us; the launch traced here: 350 us
  blocking collectives  173 us (49%)
  waiting for transfers between devices  88.3 us (25%)
  other arithmetic  54 us (15%)
  between operations  14.7 us (4%)
  matrix products  13.2 us (4%)
  local copies, waits for them, and re-layouts  7.38 us (2%)
    all_gather x2, blocking collectives, first_total(): return jnp.sum(lax.all_gather(gram, ('cell', 'gene')), axis=0)  89.3 us
    psum x1, blocking collectives, local(): next_basis = lax.psum(partial_value, 'cell').astype(jnp.bfloat16)  77.5 us
    reduce_scatter x1, waiting for transfers between devices, local(): lax.psum_scatter(loadings_of(final_rows), 'cell', scatter_dimension=1, ti...  71.8 us
    reduce_scatter x2, waiting for transfers between devices, merge_halves(): lax.psum_scatter(partial_scores, 'gene', scatter_dimension=1, tiled=True)  16.4 us
    scatter-add x2, other arithmetic, scores_of(): jax.ops.segment_sum(products, row_target, num_segments=row_blocks + 1)  14.1 us
    scatter-add x2, other arithmetic, loadings_of(): jax.ops.segment_sum(products, col_target, num_segments=gene_blocks + 1)  14.1 us
    another operation x6, other arithmetic, orthonormal(): lower_one = jnp.linalg.cholesky(first)  13 us
    another operation x4, other arithmetic, solve_lower(): return lax.linalg.triangular_solve(lower, right, left_side=True, lower=True)  11.1 us
  transfers between devices with their start and end apart: 3, of which 3 were waited for; matrix products, arithmetic and copies ran while one was open for 0% of the time, Pallas kernels for 0%

profile of v1, /device:TPU:0, one launch (start us, length us, event | category | flops | bytes accessed | tf_op | source)
XLA Modules:
  0.0 350.2 jit_solution(892566930034612232)
XLA Ops:
  7.2 0.0 copy-start
  7.2 0.0 copy-start.3
  7.2 0.0 copy-start.4
  7.2 0.0 reduce-scatter.4.cloned.1.call-start
  7.2 0.8 compare_select_fusion
  8.0 0.7 compare_and_fusion
  8.7 1.0 copy_bitcast_fusion.5
  10.4 0.7 gather_fusion
  11.1 0.0 copy-done.3
  11.2 0.0 copy-done.4
  11.2 0.0 copy-done
  11.2 2.9 fusion.6
  14.1 7.1 %scatter_fusion = f32[9,64,128]{2,1,0:T(8,128)S(1)} fusion(f32[9,64,128]{2,1,0:T(8,128)S(1)} %broadcast.69.clone, s32[64]{0:T(128)S(1)} %get-tuple-element.8, f32[64,64,128]{2,1,0:T(8,128)} %fusion.6), kind=kCustom, calls=%fused_computation.4 | custom fusion | flops 524288 | bytes 6291712 | tf_op jit(solution)/shard_map/scatter-add | solution.py:51
  21.2 0.7 copy_bitcast_fusion.3
  21.9 0.0 reduce-scatter.4.cloned.1.call-update
  21.9 0.0 reduce-scatter.6.cloned.1.call-start
  22.0 10.5 %reduce-scatter.4.cloned.1.call-done = f32[64,512]{1,0:T(8,128)} async-done(((f32[64,1024]{1,0:T(8,128)}), f32[64,512]{1,0:T(8,128)}) %reduce-scatter.4.cloned.1.call-update) | async-done | bytes 131088 | tf_op jit(solution)/shard_map/reduce_scatter | solution.py:44
  32.5 0.0 copy-start.1
  32.5 1.3 fusion.40
  33.8 44.7 %all-gather = f32[2048,64]{1,0:T(8,128)S(1)} all-gather(f32[64,64]{1,0:T(8,128)S(1)} %fusion.40), channel_id=2, replica_groups=mesh['cell'=16,'gene'=2] {'cell','gene'}, dimensions={0}, use_global_device_ids=true | all-gather | bytes 540672 | tf_op jit(solution)/shard_map/all_gather | solution.py:41
  78.5 0.1 reduce_sum.18
  78.6 0.1 copy.25
  78.7 5.8 %cholesky.44 = f32[64,64]{1,0:T(8,128)S(1)} custom-call(f32[64,64]{1,0:T(8,128)S(1)} %fusion.30), custom_call_target="Cholesky" | custom-call | tf_op jit(solution)/shard_map/jit(cholesky)/cholesky | solution.py:21
  84.6 0.6 compare_reduce_fusion.1
  85.2 0.7 fusion.24
  85.9 4.9 %custom-call.6 = f32[1,64,64]{1,2,0:T(8,128)S(1)} custom-call(f32[1,64,64]{2,1,0:T(8,128)S(1)} %fusion.24), custom_call_target="InvertDiagBlocksLowerTriangular" | custom-call | tf_op jit(solution)/shard_map/triangular_solve/custom-call.0 | solution.py:10
  90.8 0.0 copy-done.1
  90.8 0.3 convolution_convert_fusion
  91.1 1.9 all_gather.23
  93.0 0.7 gather_fusion.1
  93.8 2.1 fusion.4
  95.9 7.1 %scatter_fusion.1 = f32[17,64,128]{2,1,0:T(8,128)S(1)} fusion(f32[17,64,128]{2,1,0:T(8,128)S(1)} %broadcast.70.clone, s32[64]{0:T(128)S(1)} %get-tuple-element.9, f32[64,64,128]{2,1,0:T(8,128)} %fusion.4), kind=kCustom, calls=%fused_computation.5 | custom fusion | flops 524288 | bytes 6291712 | tf_op jit(solution)/shard_map/scatter-add | solution.py:59
  103.0 77.5 %all-reduce.1 = bf16[64,2048]{1,0:T(8,128)(2,1)S(1)} all-reduce(f32[64,2048]{1,0:T(8,128)S(1)} %copy_bitcast_fusion.1), channel_id=1, replica_groups=mesh['cell'=16,'gene'=2] {'cell'}, use_global_device_ids=true, to_apply=%region_6.11 | all-reduce | flops 131072 | bytes 786432 | tf_op jit(solution)/shard_map/psum | solution.py:68
  180.5 0.1 copy_bitcast_fusion.4
  180.6 0.8 gather_fusion.2
  181.3 2.9 fusion.2
  184.3 7.1 %scatter_fusion.2 = f32[9,64,128]{2,1,0:T(8,128)S(1)} fusion(f32[9,64,128]{2,1,0:T(8,128)S(1)} %broadcast.69, s32[64]{0:T(128)S(1)} %get-tuple-element.8, f32[64,64,128]{2,1,0:T(8,128)} %fusion.2), kind=kCustom, calls=%fused_computation.6 | custom fusion | flops 524288 | bytes 6291712 | tf_op jit(solution)/shard_map/scatter-add | solution.py:51
  191.3 0.7 copy_bitcast_fusion.2
  192.0 0.0 reduce-scatter.6.cloned.1.call-update
  192.1 0.0 reduce-scatter.8.cloned.1.call-start
  192.1 5.9 %reduce-scatter.6.cloned.1.call-done = f32[64,512]{1,0:T(8,128)} async-done(((f32[64,1024]{1,0:T(8,128)}), f32[64,512]{1,0:T(8,128)}) %reduce-scatter.6.cloned.1.call-update) | async-done | bytes 131088 | tf_op jit(solution)/shard_map/reduce_scatter | solution.py:44
  198.0 0.0 copy-start.2
  198.0 1.3 fusion.41
  199.3 44.7 %all-gather.1 = f32[2048,64]{1,0:T(8,128)S(1)} all-gather(f32[64,64]{1,0:T(8,128)S(1)} %fusion.41), channel_id=3, replica_groups=mesh['cell'=16,'gene'=2] {'cell','gene'}, dimensions={0}, use_global_device_ids=true | all-gather | bytes 540672 | tf_op jit(solution)/shard_map/all_gather | solution.py:41
  244.0 0.1 reduce_sum.19
  244.1 0.1 copy.30
  244.2 5.8 %cholesky.55 = f32[64,64]{1,0:T(8,128)S(1)} custom-call(f32[64,64]{1,0:T(8,128)S(1)} %fusion.28), custom_call_target="Cholesky" | custom-call | tf_op jit(solution)/shard_map/jit(cholesky)/cholesky | solution.py:21
  250.0 0.6 compare_reduce_fusion
  250.7 0.7 fusion.25
  251.4 4.9 %custom-call.7 = f32[1,64,64]{1,2,0:T(8,128)S(1)} custom-call(f32[1,64,64]{2,1,0:T(8,128)S(1)} %fusion.25), custom_call_target="InvertDiagBlocksLowerTriangular" | custom-call | tf_op jit(solution)/shard_map/triangular_solve/custom-call.0 | solution.py:10
  256.2 0.0 copy-done.2
  256.3 0.3 fusion.39
  256.6 1.9 all_gather.27
  258.5 0.7 gather_fusion.3
  259.3 2.1 fusion
  261.4 7.1 %scatter_fusion.3 = f32[17,64,128]{2,1,0:T(8,128)S(1)} fusion(f32[17,64,128]{2,1,0:T(8,128)S(1)} %broadcast.70, s32[64]{0:T(128)S(1)} %get-tuple-element.9, f32[64,64,128]{2,1,0:T(8,128)} %fusion), kind=kCustom, calls=%fused_computation.7 | custom fusion | flops 524288 | bytes 6291712 | tf_op jit(solution)/shard_map/scatter-add | solution.py:59
  268.5 0.8 copy_bitcast_fusion
  269.3 0.0 reduce-scatter.8.cloned.1.call-update
  269.3 1.9 all_gather.26
  271.2 71.8 %reduce-scatter.8.cloned.1.call-done = f32[64,128]{1,0:T(8,128)} async-done(((f32[64,2048]{1,0:T(8,128)}), f32[64,128]{1,0:T(8,128)}) %reduce-scatter.8.cloned.1.call-update) | async-done | bytes 32784 | tf_op jit(solution)/shard_map/reduce_scatter | solution.py:77
  343.1 0.7 copy.59
  (16 shorter events, 0.3 us)
Async XLA Ops:
  7.2 4.0 %copy-start = (bf16[1,64,128,128]{3,2,1,0:T(8,128)(2,1)S(1)}, bf16[1,64,128,128]{3,2,1,0:T(8,128)(2,1)}, u32[]{:S(2)}) copy-start(bf16[1,64,128,128]{3,2,1,0:T(8,128)(2,1)} %param.12) | copy-start | bytes 6291460
  7.2 4.0 %copy-start.3 = (s32[1,64]{1,0:T(1,128)S(1)}, s32[1,64]{1,0:T(1,128)}, u32[]{:S(2)}) copy-start(s32[1,64]{1,0:T(1,128)} %param.14) | copy-start | bytes 772
  7.2 4.0 %copy-start.4 = (s32[1,64]{1,0:T(1,128)S(1)}, s32[1,64]{1,0:T(1,128)}, u32[]{:S(2)}) copy-start(s32[1,64]{1,0:T(1,128)} %param.13) | copy-start | bytes 772
  7.2 25.3 %reduce-scatter.4.cloned.1.call-start = ((), (), s32[]{:S(2)}) async-start(), calls=%async_computation.3 | async-start | bytes 393216 | tf_op jit(solution)/shard_map/reduce_scatter | solution.py:44
  21.9 176.1 %reduce-scatter.6.cloned.1.call-start = ((), (), s32[]{:S(2)}) async-start(), calls=%async_computation.4 | async-start | bytes 393216 | tf_op jit(solution)/shard_map/reduce_scatter | solution.py:44
  32.5 58.3 %copy-start.1 = (f32[64,512]{1,0:T(8,128)S(1)}, f32[64,512]{1,0:T(8,128)}, u32[]{:S(2)}) copy-start(f32[64,512]{1,0:T(8,128)} %reduce-scatter.4.cloned.1.call-done) | copy-start | bytes 393220
  192.1 151.0 %reduce-scatter.8.cloned.1.call-start = ((), (), s32[]{:S(2)}) async-start(), calls=%async_computation.5 | async-start | bytes 557056 | tf_op jit(solution)/shard_map/reduce_scatter | solution.py:77
  198.0 58.3 %copy-start.2 = (f32[64,512]{1,0:T(8,128)S(1)}, f32[64,512]{1,0:T(8,128)}, u32[]{:S(2)}) copy-start(f32[64,512]{1,0:T(8,128)} %reduce-scatter.6.cloned.1.call-done) | copy-start | bytes 393220
Sparse Core Ops, SparseCore 0:
  22.0 10.4 reduce-scatter.3
  192.2 5.7 reduce-scatter.5
  269.5 73.5 reduce-scatter.7
